TPU v7x, 8 devices: a whole 2x2x1 slice. The times are simulated.
8 devices in a mesh: dp: 1 (over z), tp: 8 (over y, x, core).
Axes of the slice: x: 2, y: 2, z: 1, core: 2. Of those that a mesh axis runs over, the one named last changes fastest.
Arguments:
- x_in: bfloat16 [1536, 2048], P('dp')
- g_norm: bfloat16 [2048], replicated
- w_q: bfloat16 [2048, 2048], P(None, 'tp')
- w_k: bfloat16 [2048, 1024], replicated
- w_v: bfloat16 [2048, 1024], replicated
- w_o: bfloat16 [2048, 2048], P('tp')
- w_gate: bfloat16 [2048, 6144], P(None, 'tp')
- w_up: bfloat16 [2048, 6144], P(None, 'tp')
- w_down: bfloat16 [6144, 2048], P('tp')
Outputs:
- output 1: bfloat16 [1536, 2048], P('dp')
- output 2: bfloat16 [1536, 8, 128], P('dp', 'tp')
- output 3: bfloat16 [1536, 8, 128], P('dp', 'tp')
All inputs are finite; a program needn't handle non-finite values.
Results may differ from a plain program's by a relative error of at most 0.0113708.
Values are sent between devices in bfloat16 or wider.
A program may use at most 1 GiB of HBM per device.

v0:
```python
import math
import numpy as np
import jax
import jax.numpy as jnp
from jax import lax
from jax.experimental import pallas as pl
from jax.experimental.pallas import tpu as pltpu
from jax.sharding import PartitionSpec as P

HEAD_DIM = 128
ROPE_BASE = 500000.0
NORM_EPS = 1e-5
TOKENS = 1536
WIDTH = 2048
QCOLS = 256
FFCOLS = 768
ROWS = 256
BLOCKS = TOKENS // ROWS
KDOWN = QCOLS + FFCOLS
HALF = ROWS // 2
UNITS = TOKENS // HALF
STAGE_SLOTS = {
    "b": (3, 3, 6, 7, 9, 11, 12, 15, 17, 22, 22, 29),
    "c": (5, 6, 10, 10, 12, 17, 17, 17, 25, 35, 35, 48),
    "d": (7, 9, 21, 21, 21, 26, 31, 32, 35, 38, 41, 59),
    "e": (24, 26, 35, 51, 51, 56, 59, 61, 62, 66, 71, 73),
}
SCORE_SCALE = math.log2(math.e) / math.sqrt(HEAD_DIM)
F32 = jnp.float32
BF16 = jnp.bfloat16
MESH = pl.DeviceIdType.MESH

D2D_FIRST, D2D_SECOND, RED_PASS, RED_STAY, RED_TWO, GAT_ONE, GAT_OWN, GAT_PASS, OUT_FIRST, OUT_SECOND = range(10)


def rope_table():
    inv_freq = np.float32(ROPE_BASE) ** (-np.arange(0, HEAD_DIM, 2, dtype=np.float32) / np.float32(HEAD_DIM))
    angles = np.arange(TOKENS, dtype=np.float32)[:, None] * inv_freq.astype(np.float32)[None, :]
    angles = angles.astype(np.float64)
    return np.concatenate([np.cos(angles), np.sin(angles)], axis=1).astype(np.float32)


def layer_kernel(x_hbm, g_hbm, wq_hbm, wk_hbm, wv_hbm, wo_hbm, wg_hbm, wu_hbm, wd_hbm, tab_hbm,
                 y_v, k_v, v_v,
                 x_v, g_v, gf_v, wqkv_v, wg_v, wu_v, wod_v, tab_v,
                 a_v, q_v, s_v, p_v, om_v,
                 d2d_src, d2d_dst, h_send, h_keep, r1_dst, p_send, r2_dst,
                 x_sem, w_sem, ssem, pair_sem, link_sem, out_sem):
    me = lax.axis_index('tp')
    core = lax.rem(me, 2)
    xpos = lax.rem(me // 2, 2)
    ypos = me // 4
    sibling = me + 1 - 2 * core
    xpeer = me + 2 - 4 * xpos
    ypeer = me + 4 - 8 * ypos
    p1 = xpos + core * (ypos - xpos)
    p2 = ypos + core * (xpos - ypos)
    n1 = xpeer + core * (ypeer - xpeer)
    n2 = ypeer + core * (xpeer - ypeer)

    def rows_of(b):
        return pl.ds(pl.multiple_of(b * ROWS, ROWS), ROWS)

    def load(src, dst, index):
        return pltpu.make_async_copy(src, dst, w_sem.at[index])

    def load_x(b):
        return pltpu.make_async_copy(x_hbm.at[rows_of(b), :], x_v.at[rows_of(b), :], x_sem.at[b])

    def load_first(n):
        rows = pl.ds(n * 64, 64)
        return pltpu.make_async_copy(x_hbm.at[rows, :], x_v.at[rows, :], x_sem.at[0 if n == 0 else BLOCKS - 1 + n])

    kv_cols = pl.ds(pl.multiple_of(me * HEAD_DIM, HEAD_DIM), HEAD_DIM)
    early, late = pl.ds(0, 2 * ROWS), pl.ds(2 * ROWS, TOKENS - 2 * ROWS)
    load_g = load(g_hbm, g_v, 0)
    load_qkv = [
        load(wk_hbm.at[:, kv_cols], wqkv_v.at[:, pl.ds(QCOLS, HEAD_DIM)], 1),
        load(wv_hbm.at[:, kv_cols], wqkv_v.at[:, pl.ds(QCOLS + HEAD_DIM, HEAD_DIM)], 1),
        load(wq_hbm, wqkv_v.at[:, pl.ds(0, QCOLS)], 1),
    ]
    wait_qkv = load(wqkv_v, wqkv_v, 1)
    load_early = load(tab_hbm.at[early, :], tab_v.at[early, :], 2)
    load_gu, wait_gu = [], []
    for n in range(FFCOLS // 256):
        tile = pl.ds(n * 256, 256)
        load_gu.append((load(wg_hbm.at[:, tile], wg_v.at[:, tile], 3 + n), load(wu_hbm.at[:, tile], wu_v.at[:, tile], 3 + n)))
        both = wg_v.at[:, pl.ds(0, 512)]
        wait_gu.append(load(both, both, 3 + n))
    load_od, wait_od = [], []
    for n, half in enumerate((1 - core, core)):
        cols = pl.ds(pl.multiple_of(half * 1024, 1024), 1024)
        load_od.append((load(wo_hbm.at[:, cols], wod_v.at[pl.ds(0, QCOLS), cols], 6 + n),
                        load(wd_hbm.at[:, cols], wod_v.at[pl.ds(QCOLS, FFCOLS), cols], 6 + n)))
        wait_od.append(load(wod_v.at[:, cols], wod_v.at[:, cols], 6 + n))
    load_tab = load(tab_hbm.at[late, :], tab_v.at[late, :], 8)

    load_g.start()
    for n in range(4):
        load_first(n).start()
    for copy in load_qkv:
        copy.start()
    load_early.start()

    barrier = pltpu.get_barrier_semaphore()
    for peer in (sibling, xpeer, ypeer):
        pl.semaphore_signal(barrier, inc=1, device_id={'tp': peer}, device_id_type=MESH)

    def remote(kind, src, dst, recv, peer):
        return pltpu.make_async_remote_copy(src_ref=src, dst_ref=dst, send_sem=ssem.at[kind], recv_sem=recv,
                                            device_id={'tp': peer}, device_id_type=MESH)

    mine = core * 4 + p1 * 2
    other = core * 4 + (1 - p1) * 2

    def half_rows(u):
        return pl.ds(pl.multiple_of(u * HALF, HALF), HALF)

    def y_part(u, piece, count):
        return y_v.at[half_rows(u), pl.ds(pl.multiple_of(piece * 256, 256), count * 256)]

    def pair_copy(kind, b):
        units = pl.ds(2 * b, 2)
        return remote(kind, d2d_src.at[kind, units], d2d_dst.at[kind, units], pair_sem.at[kind, b], sibling)

    def quarter_cols(index):
        return pl.ds(pl.multiple_of(index * 256, 256), 256)

    def copy_of(kind, u):
        if kind in (OUT_FIRST, OUT_SECOND):
            part = y_part(u, mine if kind == OUT_FIRST else other, 2)
            return remote(kind, part, part, out_sem.at[kind - OUT_FIRST], sibling)
        sem = link_sem.at[kind - RED_PASS, u]
        if kind in (RED_PASS, RED_STAY):
            cols = quarter_cols(1 - p2 if kind == RED_PASS else p2)
            return remote(kind, h_send.at[u, :, cols], r1_dst.at[u, :, cols], sem, n1)
        if kind == RED_TWO:
            return remote(kind, p_send.at[u], r2_dst.at[u], sem, n2)
        part = y_part(u, mine + (1 - p2 if kind == GAT_PASS else p2), 1)
        return remote(kind, part, part, sem, n2 if kind == GAT_ONE else n1)

    def all_of(kind):
        small = RED_PASS <= kind <= GAT_PASS
        src, dst = (p_send, r2_dst) if small else (h_send, r1_dst)
        return remote(kind, src, dst, out_sem.at[1 if kind == OUT_SECOND else 0], sibling)

    def norm_rows(b, r):
        x_f = x_v[pl.ds(pl.multiple_of(b * ROWS + r * 16, 16), 16), :].astype(F32)
        inv = lax.rsqrt(jnp.mean(x_f * x_f, axis=-1, keepdims=True) + NORM_EPS)
        gain = jnp.concatenate([gf_v[...], gf_v[...]], axis=0)
        a_v[b % 2, pl.ds(r * 16, 16), :] = (x_f * inv * gain).astype(BF16)

    def first_norm():
        load_g.wait()
        gf_v[...] = jnp.broadcast_to(g_v[...].astype(F32)[None, :], (8, WIDTH))
        for n in range(4):
            load_first(n).wait()
            if n < 3:
                for copy in load_gu[n]:
                    copy.start()
            for r in range(n * 4, n * 4 + 4):
                norm_rows(0, r)
        wait_qkv.wait()
        load_early.wait()
        pl.semaphore_wait(barrier, 3)

    def project(b):
        @pl.when(b == 2)
        def _():
            load_tab.wait()

        tab = tab_v[rows_of(b), :]
        swapped = pltpu.roll(tab, HEAD_DIM // 2, 1)
        low = lax.broadcasted_iota(jnp.int32, tab.shape, 1) < HEAD_DIM // 2
        cos = jnp.where(low, tab, swapped)
        sin = jnp.where(low, -swapped, tab)
        qkv = jnp.dot(a_v[lax.rem(b, 2)], wqkv_v[...], preferred_element_type=F32)

        def rope(h):
            return (h * cos + pltpu.roll(h, HEAD_DIM // 2, 1) * sin).astype(BF16)

        q_v[pl.ds(0, ROWS), :] = rope(qkv[:, 0:128])
        q_v[pl.ds(ROWS, ROWS), :] = rope(qkv[:, 128:256])
        k_v[rows_of(b), :] = rope(qkv[:, 256:384])
        v_v[rows_of(b), :] = qkv[:, 384:512].astype(BF16)

    def attention(b):
        def tile(j):
            return pl.ds(j * ROWS, ROWS)

        heads = range(2)
        peak, total, shift = [None] * 2, [None] * 2, [None] * 2
        for j in range(b + 1):
            for h in heads:
                q = q_v[pl.ds(h * ROWS, ROWS), :]
                s = lax.dot_general(q, k_v[tile(j), :], (((1,), (1,)), ((), ())), preferred_element_type=F32) * SCORE_SCALE
                if j == b:
                    qpos = lax.broadcasted_iota(jnp.int32, (ROWS, ROWS), 0)
                    kpos = lax.broadcasted_iota(jnp.int32, (ROWS, ROWS), 1)
                    s = jnp.where(kpos <= qpos, s, -1e30)
                s_v[h, :, tile(j)] = s
                pair = jnp.maximum(s[:, :128], s[:, 128:])
                peak[h] = pair if j == 0 else jnp.maximum(peak[h], pair)
                yield
        for h in heads:
            peak[h] = jnp.max(peak[h], axis=1, keepdims=True)
        for j in range(b + 1):
            for h in heads:
                e = jnp.exp2(s_v[h, :, tile(j)] - peak[h])
                pair = e[:, :128] + e[:, 128:]
                total[h] = pair if j == 0 else total[h] + pair
                yield
        for h in heads:
            shift[h] = peak[h] + jnp.log2(jnp.sum(total[h], axis=1, keepdims=True))
        for j in range(b + 1):
            for h in heads:
                p_v[h, :, tile(j)] = jnp.exp2(s_v[h, :, tile(j)] - shift[h]).astype(BF16)
                yield
        keys = pl.ds(0, (b + 1) * ROWS)
        for h in heads:
            o = jnp.dot(p_v[h, :, keys], v_v[keys, :], preferred_element_type=F32)
            om_v[:, pl.ds(h * HEAD_DIM, HEAD_DIM)] = o.astype(BF16)
            yield

    def gate_up(b):
        normed = a_v.at[b % 2]
        for n in range(FFCOLS // 256):
            if b == 0:
                wait_gu[n].wait()
            cols = pl.ds(n * 256, 256)
            gate = jnp.dot(normed[...], wg_v[:, cols], preferred_element_type=F32)
            yield
            up = jnp.dot(normed[...], wu_v[:, cols], preferred_element_type=F32)
            om_v[:, pl.ds(QCOLS + n * 256, 256)] = (gate * (1.0 / (1.0 + jnp.exp(-gate))) * up).astype(BF16)
            yield

    def next_norm(b):
        for r in range(ROWS // 16):
            norm_rows(b + 1, r)
            yield

    def mix_block(b):
        works = [(gate_up(b), [k / 6 for k in range(6)])]
        count = 6 * (b + 1) + 2
        works.append((attention(b), [k / count for k in range(count)]))
        if b == 0:
            for copy in load_od[0]:
                copy.start()
            load_x(1).start()
            for copy in load_od[1]:
                copy.start()
        elif b < BLOCKS - 1:
            count = ROWS // 16
            load_x(b + 1).wait()
            works.append((next_norm(b), [k / count for k in range(count)]))
        turns = sorted((turn, index) for index, (_, turns) in enumerate(works) for turn in turns)
        for _, index in turns:
            next(works[index][0])
        for work, _ in works:
            for _ in work:
                pass
        if b == 0:
            wait_od[0].wait()
        pair_product(D2D_FIRST, 1 - p2, b)
        pair_copy(D2D_FIRST, b).start()

    def mix(i):
        for b in range(BLOCKS):
            @pl.when(i == b)
            def _():
                mix_block(b)

    def down(half, quarter):
        cols = pl.ds(pl.multiple_of(half * 1024 + quarter * 512, 512), 512)
        return jnp.dot(om_v[...], wod_v[:, cols], preferred_element_type=F32)

    def pair_product(kind, quarter, b):
        part = down(1 - core, quarter).astype(BF16)
        for s in range(2):
            d2d_src[kind, 2 * b + s] = part[s * HALF:(s + 1) * HALF]

    def down_rest(i):
        def rest(b, first):
            norms = iter(range(ROWS // 16) if first else ())

            def some_norms():
                for _ in range(6):
                    for r in norms:
                        norm_rows(1, r)
                        break

            pair_product(D2D_SECOND, p2, b)
            some_norms()
            send = down(core, 1 - p1)
            some_norms()
            keep = down(core, p1)
            some_norms()
            for s in range(2):
                h_keep[2 * b + s] = keep[s * HALF:(s + 1) * HALF]
            pair_copy(D2D_SECOND, b).start()
            with jax.named_scope("recv"):
                pair_copy(D2D_FIRST, b).wait_recv()
            for s in range(2):
                u = 2 * b + s
                h_send[u] = (send[s * HALF:(s + 1) * HALF] + d2d_dst[0, u].astype(F32)).astype(BF16)
                copy_of(RED_PASS, u).start()
                copy_of(RED_STAY, u).start()

        @pl.when(i == 0)
        def _():
            wait_od[1].wait()
            load_x(1).wait()
            rest(0, True)
            load_tab.start()
            for n in range(2, BLOCKS):
                load_x(n).start()

        @pl.when(i > 0)
        def _():
            rest(i, False)

    def stage_b(u):
        with jax.named_scope("recv"):
            copy_of(RED_PASS, u).wait_recv()
            if u % 2 == 0:
                pair_copy(D2D_SECOND, u // 2).wait_recv()
        p_send[u] = partial(u, quarter_cols(1 - p2)).astype(BF16)
        copy_of(RED_TWO, u).start()

    def partial(u, cols):
        return h_keep[u, :, cols] + d2d_dst[1, u, :, cols].astype(F32) + r1_dst[u, :, cols].astype(F32)

    def stage_c(u):
        with jax.named_scope("recv"):
            copy_of(RED_STAY, u).wait_recv()
            copy_of(RED_TWO, u).wait_recv()
        cols = quarter_cols(mine + p2)
        x_f = x_v[half_rows(u), cols].astype(F32)
        y_v[half_rows(u), cols] = (x_f + (partial(u, quarter_cols(p2)) + r2_dst[u].astype(F32))).astype(BF16)
        copy_of(GAT_ONE, u).start()
        copy_of(GAT_OWN, u).start()

    def stage_d(u):
        with jax.named_scope("recv"):
            copy_of(GAT_ONE, u).wait_recv()
        copy_of(GAT_PASS, u).start()
        copy_of(OUT_FIRST, u).start()

    def stage_e(u):
        with jax.named_scope("recv"):
            copy_of(GAT_OWN, u).wait_recv()
            copy_of(GAT_PASS, u).wait_recv()
        copy_of(OUT_SECOND, u).start()

    stages = {"b": stage_b, "c": stage_c, "d": stage_d, "e": stage_e}

    slots = {}
    for name in "bcde":
        for u in range(UNITS):
            slots.setdefault(STAGE_SLOTS[name][u], []).append((name, u))

    def communicate(slot):
        for name, u in slots.get(slot, ()):
            with jax.named_scope("stage_" + name):
                stages[name](u)

    def next_project(i):
        @pl.when(i < BLOCKS - 1)
        def _():
            project(i + 1)

    def step(i, carry):
        for point, part in enumerate((mix, down_rest, next_project)):
            with jax.named_scope(part.__name__):
                part(i)
            for b in range(BLOCKS):
                if 3 * b + point in slots:
                    @pl.when(i == b)
                    def _():
                        communicate(3 * b + point)

        return carry

    with jax.named_scope("first"):
        first_norm()
        project(0)
    lax.fori_loop(0, BLOCKS, step, 0)
    for slot in range(3 * BLOCKS, max(slots) + 1):
        communicate(slot)

    with jax.named_scope("finish"):
        for kind in (OUT_FIRST, OUT_SECOND):
            all_of(kind).wait_recv()
        for kind in range(10):
            all_of(kind).wait_send()


def store_kernel(y_v, k_v, v_v, y_out, k_out, v_out, sem):
    copies = [pltpu.make_async_copy(k_v, k_out, sem.at[0]), pltpu.make_async_copy(v_v, v_out, sem.at[1])]
    for b in range(BLOCKS):
        rows = pl.ds(b * ROWS, ROWS)
        copies.append(pltpu.make_async_copy(y_v.at[rows, :], y_out.at[rows, :], sem.at[2 + b]))
    for copy in copies:
        copy.start()
    for copy in copies:
        copy.wait()


def solution(mesh):
    table = rope_table()

    def local_layer(x_in, g_norm, w_q, w_k, w_v, w_o, w_gate, w_up, w_down):
        any_spec = pl.BlockSpec(memory_space=pl.ANY)
        y, k, v = pl.pallas_call(
            layer_kernel,
            out_shape=(pltpu.VMEM((TOKENS, WIDTH), BF16), pltpu.VMEM((TOKENS, HEAD_DIM), BF16), pltpu.VMEM((TOKENS, HEAD_DIM), BF16)),
            in_specs=[any_spec] * 10,
            out_specs=(pl.BlockSpec(memory_space=pltpu.VMEM),) * 3,
            scratch_shapes=[
                pltpu.VMEM((TOKENS, WIDTH), BF16),
                pltpu.VMEM((WIDTH,), BF16),
                pltpu.VMEM((8, WIDTH), F32),
                pltpu.VMEM((WIDTH, QCOLS + 2 * HEAD_DIM), BF16),
                pltpu.VMEM((WIDTH, FFCOLS), BF16),
                pltpu.VMEM((WIDTH, FFCOLS), BF16),
                pltpu.VMEM((KDOWN, WIDTH), BF16),
                pltpu.VMEM((TOKENS, HEAD_DIM), F32),
                pltpu.VMEM((2, ROWS, WIDTH), BF16),
                pltpu.VMEM((2 * ROWS, HEAD_DIM), BF16),
                pltpu.VMEM((2, ROWS, TOKENS), F32),
                pltpu.VMEM((2, ROWS, TOKENS), BF16),
                pltpu.VMEM((ROWS, KDOWN), BF16),
                pltpu.VMEM((2, UNITS, HALF, 512), BF16),
                pltpu.VMEM((2, UNITS, HALF, 512), BF16),
                pltpu.VMEM((UNITS, HALF, 512), BF16),
                pltpu.VMEM((UNITS, HALF, 512), F32),
                pltpu.VMEM((UNITS, HALF, 512), BF16),
                pltpu.VMEM((UNITS, HALF, 256), BF16),
                pltpu.VMEM((UNITS, HALF, 256), BF16),
                pltpu.SemaphoreType.DMA((BLOCKS + 3,)),
                pltpu.SemaphoreType.DMA((9,)),
                pltpu.SemaphoreType.DMA((10,)),
                pltpu.SemaphoreType.DMA((2, BLOCKS)),
                pltpu.SemaphoreType.DMA((6, UNITS)),
                pltpu.SemaphoreType.DMA((2,)),
            ],
            compiler_params=pltpu.CompilerParams(collective_id=0, has_side_effects=True, vmem_limit_bytes=67043328 - 8 * 1024 * 1024),
        )(x_in, g_norm, w_q, w_k, w_v, w_o, w_gate, w_up, w_down, jnp.asarray(table))
        y, k, v = pl.pallas_call(
            store_kernel,
            out_shape=(jax.ShapeDtypeStruct((TOKENS, WIDTH), BF16), jax.ShapeDtypeStruct((TOKENS, HEAD_DIM), BF16),
                       jax.ShapeDtypeStruct((TOKENS, HEAD_DIM), BF16)),
            in_specs=[any_spec] * 3,
            out_specs=(any_spec,) * 3,
            scratch_shapes=[pltpu.SemaphoreType.DMA((2 + BLOCKS,))],
            compiler_params=pltpu.CompilerParams(vmem_limit_bytes=1024 * 1024),
        )(*(pltpu.with_memory_space_constraint(part, pltpu.VMEM) for part in (y, k, v)))
        return y, k.reshape(TOKENS, 1, HEAD_DIM), v.reshape(TOKENS, 1, HEAD_DIM)

    return jax.shard_map(local_layer, mesh=mesh, in_specs=(P('dp', None), P(None), P(None, 'tp'), P(None, None), P(None, None), P('tp', None), P(None, 'tp'), P(None, 'tp'), P('tp', None)), out_specs=(P('dp', None), P('dp', 'tp', None), P('dp', 'tp', None)), check_vma=False)
```

profile of v0, /device:TPU:0, one launch (start us, length us, event | category | flops | bytes accessed | tf_op | source)
XLA Modules:
  0.0 69.4 jit_solution(3180076661840554488)
XLA Ops:
  0.6 65.7 %shard_map.121 = (bf16[1536,2048]{1,0:T(8,128)(2,1)S(1)}, bf16[1536,128]{1,0:T(8,128)(2,1)S(1)}, bf16[1536,128]{1,0:T(8,128)(2,1)S(1)}) custom-call(bf16[1536,2048]{1,0:T(8,128)(2,1)} %x_hbm.1, bf16[2048]{0:T(1024)(128)(2,1)} %g_hbm.1, bf16[2048,256]{1,0:T(8,128)(2,1)} %wq_hbm.1, bf16[2048,1024]{1,0:T(8,128)(2,1)} %wk_hbm.1, bf16[2048,1024]{1,0:T(8,128)(2,1)} %wv_hbm.1, ...), custom_call_target="tpu_custom_call" | custom-call | tf_op jit(solution)/shard_map/pallas_call | solution.py:414
  66.4 3.0 %shard_map.122 = (bf16[1536,2048]{1,0:T(8,128)(2,1)}, bf16[1536,128]{1,0:T(8,128)(2,1)}, bf16[1536,128]{1,0:T(8,128)(2,1)}) custom-call(bf16[1536,2048]{1,0:T(8,128)(2,1)S(1)} %get-tuple-element.9.y_v, bf16[1536,128]{1,0:T(8,128)(2,1)S(1)} %get-tuple-element.10.k_v, bf16[1536,128]{1,0:T(8,128)(2,1)S(1)} %get-tuple-element.11.v_v), custom_call_target="tpu_custom_call" | custom-call | tf_op jit(solution)/shard_map/pallas_call | solution.py:449
where the time goes:
time: 69.5 us; the launch traced here: 69.4 us
  Pallas kernels  68.7 us (99%)
    pallas_call x1, Pallas kernels, local_layer(): pl.pallas_call(layer_kernel, out_shape=(pltpu.VMEM((TOKENS, WIDTH), BF16)...  65.7 us
    pallas_call x1, Pallas kernels, local_layer(): pl.pallas_call(store_kernel, out_shape=(jax.ShapeDtypeStruct((TOKENS, WID...  3 us

commit v1 on v0

--- a/solution.py
+++ b/solution.py
@@ -20,17 +20,17 @@
 HALF = ROWS // 2
 UNITS = TOKENS // HALF
 STAGE_SLOTS = {
-    "b": (3, 3, 6, 7, 9, 11, 12, 15, 17, 22, 22, 29),
-    "c": (5, 6, 10, 10, 12, 17, 17, 17, 25, 35, 35, 48),
-    "d": (7, 9, 21, 21, 21, 26, 31, 32, 35, 38, 41, 59),
-    "e": (24, 26, 35, 51, 51, 56, 59, 61, 62, 66, 71, 73),
+    "b": (3, 3, 6, 6, 9, 9, 12, 17, 23, 27, 27, 32),
+    "c": (5, 5, 9, 11, 13, 17, 20, 23, 39, 39, 40, 46),
+    "d": (6, 8, 13, 14, 17, 38, 43, 44, 45, 56, 57, 60),
+    "e": (9, 25, 27, 34, 42, 56, 63, 64, 83, 88, 90, 94),
 }
 SCORE_SCALE = math.log2(math.e) / math.sqrt(HEAD_DIM)
 F32 = jnp.float32
 BF16 = jnp.bfloat16
 MESH = pl.DeviceIdType.MESH
 
-D2D_FIRST, D2D_SECOND, RED_PASS, RED_STAY, RED_TWO, GAT_ONE, GAT_OWN, GAT_PASS, OUT_FIRST, OUT_SECOND = range(10)
+PAIR_PASS, PAIR_STAY, PAIR_KEEP, RED_PASS, RED_STAY, RED_TWO, GAT_ONE, GAT_OWN, GAT_PASS, OUT_FIRST, OUT_SECOND = range(11)
 
 
 def rope_table():
@@ -44,7 +44,7 @@
                  y_v, k_v, v_v,
                  x_v, g_v, gf_v, wqkv_v, wg_v, wu_v, wod_v, tab_v,
                  a_v, q_v, s_v, p_v, om_v,
-                 d2d_src, d2d_dst, h_send, h_keep, r1_dst, p_send, r2_dst,
+                 d2d_src, d2d_dst, h_send, h_keep, r1_dst, p_send, r2_dst, send_v,
                  x_sem, w_sem, ssem, pair_sem, link_sem, out_sem):
     me = lax.axis_index('tp')
     core = lax.rem(me, 2)
@@ -119,12 +119,17 @@
     def y_part(u, piece, count):
         return y_v.at[half_rows(u), pl.ds(pl.multiple_of(piece * 256, 256), count * 256)]
 
+    def quarter_cols(index):
+        return pl.ds(pl.multiple_of(index * 256, 256), 256)
+
     def pair_copy(kind, b):
         units = pl.ds(2 * b, 2)
-        return remote(kind, d2d_src.at[kind, units], d2d_dst.at[kind, units], pair_sem.at[kind, b], sibling)
-
-    def quarter_cols(index):
-        return pl.ds(pl.multiple_of(index * 256, 256), 256)
+        if kind == PAIR_KEEP:
+            src, dst = d2d_src.at[1, units], d2d_dst.at[1, units]
+        else:
+            cols = quarter_cols(1 - p1 if kind == PAIR_PASS else p1)
+            src, dst = d2d_src.at[0, units, :, cols], d2d_dst.at[0, units, :, cols]
+        return remote(kind, src, dst, pair_sem.at[kind, b], sibling)
 
     def copy_of(kind, u):
         if kind in (OUT_FIRST, OUT_SECOND):
@@ -140,7 +145,7 @@
         return remote(kind, part, part, sem, n2 if kind == GAT_ONE else n1)
 
     def all_of(kind):
-        small = RED_PASS <= kind <= GAT_PASS
+        small = kind not in (PAIR_KEEP, OUT_FIRST, OUT_SECOND)
         src, dst = (p_send, r2_dst) if small else (h_send, r1_dst)
         return remote(kind, src, dst, out_sem.at[1 if kind == OUT_SECOND else 0], sibling)
 
@@ -261,8 +266,9 @@
                 pass
         if b == 0:
             wait_od[0].wait()
-        pair_product(D2D_FIRST, 1 - p2, b)
-        pair_copy(D2D_FIRST, b).start()
+        pair_product(0, 1 - p2, b)
+        pair_copy(PAIR_PASS, b).start()
+        pair_copy(PAIR_STAY, b).start()
 
     def mix(i):
         for b in range(BLOCKS):
@@ -274,10 +280,10 @@
         cols = pl.ds(pl.multiple_of(half * 1024 + quarter * 512, 512), 512)
         return jnp.dot(om_v[...], wod_v[:, cols], preferred_element_type=F32)
 
-    def pair_product(kind, quarter, b):
+    def pair_product(slot, quarter, b):
         part = down(1 - core, quarter).astype(BF16)
         for s in range(2):
-            d2d_src[kind, 2 * b + s] = part[s * HALF:(s + 1) * HALF]
+            d2d_src[slot, 2 * b + s] = part[s * HALF:(s + 1) * HALF]
 
     def down_rest(i):
         def rest(b, first):
@@ -289,22 +295,24 @@
                         norm_rows(1, r)
                         break
 
-            pair_product(D2D_SECOND, p2, b)
+            pair_product(1, p2, b)
             some_norms()
-            send = down(core, 1 - p1)
+            send_v[...] = down(core, 1 - p1)
             some_norms()
             keep = down(core, p1)
             some_norms()
             for s in range(2):
                 h_keep[2 * b + s] = keep[s * HALF:(s + 1) * HALF]
-            pair_copy(D2D_SECOND, b).start()
-            with jax.named_scope("recv"):
-                pair_copy(D2D_FIRST, b).wait_recv()
-            for s in range(2):
-                u = 2 * b + s
-                h_send[u] = (send[s * HALF:(s + 1) * HALF] + d2d_dst[0, u].astype(F32)).astype(BF16)
-                copy_of(RED_PASS, u).start()
-                copy_of(RED_STAY, u).start()
+            pair_copy(PAIR_KEEP, b).start()
+            for kind, pair, index in ((RED_PASS, PAIR_PASS, 1 - p2), (RED_STAY, PAIR_STAY, p2)):
+                with jax.named_scope("recv"):
+                    pair_copy(pair, b).wait_recv()
+                cols = quarter_cols(index)
+                for s in range(2):
+                    u = 2 * b + s
+                    h_send[u, :, cols] = (send_v[pl.ds(s * HALF, HALF), cols] + d2d_dst[0, u, :, cols].astype(F32)).astype(BF16)
+                for s in range(2):
+                    copy_of(kind, 2 * b + s).start()
 
         @pl.when(i == 0)
         def _():
@@ -323,7 +331,7 @@
         with jax.named_scope("recv"):
             copy_of(RED_PASS, u).wait_recv()
             if u % 2 == 0:
-                pair_copy(D2D_SECOND, u // 2).wait_recv()
+                pair_copy(PAIR_KEEP, u // 2).wait_recv()
         p_send[u] = partial(u, quarter_cols(1 - p2)).astype(BF16)
         copy_of(RED_TWO, u).start()
 
@@ -391,7 +399,7 @@
     with jax.named_scope("finish"):
         for kind in (OUT_FIRST, OUT_SECOND):
             all_of(kind).wait_recv()
-        for kind in range(10):
+        for kind in range(11):
             all_of(kind).wait_send()
 
 
@@ -437,10 +445,11 @@
                 pltpu.VMEM((UNITS, HALF, 512), BF16),
                 pltpu.VMEM((UNITS, HALF, 256), BF16),
                 pltpu.VMEM((UNITS, HALF, 256), BF16),
+                pltpu.VMEM((ROWS, 512), F32),
                 pltpu.SemaphoreType.DMA((BLOCKS + 3,)),
                 pltpu.SemaphoreType.DMA((9,)),
-                pltpu.SemaphoreType.DMA((10,)),
-                pltpu.SemaphoreType.DMA((2, BLOCKS)),
+                pltpu.SemaphoreType.DMA((11,)),
+                pltpu.SemaphoreType.DMA((3, BLOCKS)),
                 pltpu.SemaphoreType.DMA((6, UNITS)),
                 pltpu.SemaphoreType.DMA((2,)),
             ],

time: 69.5 us -> 70.3 us (1.012)
  Pallas kernels: 68.7 us -> 69.6 us
    pallas_call x1, Pallas kernels: 65.7 us -> 66.6 us  [local_layer(): pl.pallas_call(layer_kernel, out_shape=(pltpu.VMEM((TOKENS, WIDTH), BF16)...]
where the time goes in v1:
time: 70.3 us; the launch traced here: 70.2 us
  Pallas kernels  69.6 us (99%)
    pallas_call x1, Pallas kernels, local_layer(): pl.pallas_call(layer_kernel, out_shape=(pltpu.VMEM((TOKENS, WIDTH), BF16)...  66.6 us
    pallas_call x1, Pallas kernels, local_layer(): pl.pallas_call(store_kernel, out_shape=(jax.ShapeDtypeStruct((TOKENS, WID...  3 us

profile of v1, /device:TPU:0, one launch (start us, length us, event | category | flops | bytes accessed | tf_op | source)
XLA Modules:
  0.0 70.2 jit_solution(15567059334905425163)
XLA Ops:
  0.6 66.6 %shard_map.121 = (bf16[1536,2048]{1,0:T(8,128)(2,1)S(1)}, bf16[1536,128]{1,0:T(8,128)(2,1)S(1)}, bf16[1536,128]{1,0:T(8,128)(2,1)S(1)}) custom-call(bf16[1536,2048]{1,0:T(8,128)(2,1)} %x_hbm.1, bf16[2048]{0:T(1024)(128)(2,1)} %g_hbm.1, bf16[2048,256]{1,0:T(8,128)(2,1)} %wq_hbm.1, bf16[2048,1024]{1,0:T(8,128)(2,1)} %wk_hbm.1, bf16[2048,1024]{1,0:T(8,128)(2,1)} %wv_hbm.1, ...), custom_call_target="tpu_custom_call" | custom-call | tf_op jit(solution)/shard_map/pallas_call | solution.py:422
  67.2 3.0 %shard_map.122 = (bf16[1536,2048]{1,0:T(8,128)(2,1)}, bf16[1536,128]{1,0:T(8,128)(2,1)}, bf16[1536,128]{1,0:T(8,128)(2,1)}) custom-call(bf16[1536,2048]{1,0:T(8,128)(2,1)S(1)} %get-tuple-element.9.y_v, bf16[1536,128]{1,0:T(8,128)(2,1)S(1)} %get-tuple-element.10.k_v, bf16[1536,128]{1,0:T(8,128)(2,1)S(1)} %get-tuple-element.11.v_v), custom_call_target="tpu_custom_call" | custom-call | tf_op jit(solution)/shard_map/pallas_call | solution.py:458

commit v2 on v1

--- a/solution.py
+++ b/solution.py
@@ -20,10 +20,10 @@
 HALF = ROWS // 2
 UNITS = TOKENS // HALF
 STAGE_SLOTS = {
-    "b": (3, 3, 6, 6, 9, 9, 12, 17, 23, 27, 27, 32),
-    "c": (5, 5, 9, 11, 13, 17, 20, 23, 39, 39, 40, 46),
-    "d": (6, 8, 13, 14, 17, 38, 43, 44, 45, 56, 57, 60),
-    "e": (9, 25, 27, 34, 42, 56, 63, 64, 83, 88, 90, 94),
+    "b": (3, 3, 6, 7, 9, 11, 12, 15, 17, 22, 22, 29),
+    "c": (5, 6, 10, 10, 12, 17, 17, 17, 25, 35, 35, 48),
+    "d": (7, 9, 21, 21, 21, 26, 31, 32, 35, 38, 41, 59),
+    "e": (24, 26, 35, 51, 51, 56, 59, 61, 62, 66, 71, 73),
 }
 SCORE_SCALE = math.log2(math.e) / math.sqrt(HEAD_DIM)
 F32 = jnp.float32

time: 70.3 us -> 69.6 us (0.990)
  no operation moved by 1% of the time
where the time goes in v2:
time: 69.6 us; the launch traced here: 69.5 us
  Pallas kernels  68.9 us (99%)
    pallas_call x1, Pallas kernels, local_layer(): pl.pallas_call(layer_kernel, out_shape=(pltpu.VMEM((TOKENS, WIDTH), BF16)...  65.9 us
    pallas_call x1, Pallas kernels, local_layer(): pl.pallas_call(store_kernel, out_shape=(jax.ShapeDtypeStruct((TOKENS, WID...  3 us

profile of v2, /device:TPU:0, one launch (start us, length us, event | category | flops | bytes accessed | tf_op | source)
XLA Modules:
  0.0 69.5 jit_solution(11299939070360544696)
XLA Ops:
  0.6 65.9 %shard_map.121 = (bf16[1536,2048]{1,0:T(8,128)(2,1)S(1)}, bf16[1536,128]{1,0:T(8,128)(2,1)S(1)}, bf16[1536,128]{1,0:T(8,128)(2,1)S(1)}) custom-call(bf16[1536,2048]{1,0:T(8,128)(2,1)} %x_hbm.1, bf16[2048]{0:T(1024)(128)(2,1)} %g_hbm.1, bf16[2048,256]{1,0:T(8,128)(2,1)} %wq_hbm.1, bf16[2048,1024]{1,0:T(8,128)(2,1)} %wk_hbm.1, bf16[2048,1024]{1,0:T(8,128)(2,1)} %wv_hbm.1, ...), custom_call_target="tpu_custom_call" | custom-call | tf_op jit(solution)/shard_map/pallas_call | solution.py:422
  66.5 3.0 %shard_map.122 = (bf16[1536,2048]{1,0:T(8,128)(2,1)}, bf16[1536,128]{1,0:T(8,128)(2,1)}, bf16[1536,128]{1,0:T(8,128)(2,1)}) custom-call(bf16[1536,2048]{1,0:T(8,128)(2,1)S(1)} %get-tuple-element.9.y_v, bf16[1536,128]{1,0:T(8,128)(2,1)S(1)} %get-tuple-element.10.k_v, bf16[1536,128]{1,0:T(8,128)(2,1)S(1)} %get-tuple-element.11.v_v), custom_call_target="tpu_custom_call" | custom-call | tf_op jit(solution)/shard_map/pallas_call | solution.py:458
